TPU v7x, 128 devices: a whole 4x4x4 slice. The times are simulated.
128 devices in a mesh: replica: 16 (over x, z), tensor: 8 (over y, core).
Axes of the slice: x: 4, y: 4, z: 4, core: 2. Of those that a mesh axis runs over, the one named last changes fastest.
Arguments:
- queries: bfloat16 [1024, 8192], P('replica', 'tensor'), may hold values from -18 to 18
- kv_new: bfloat16 [1024, 2, 1024], P('replica', None, 'tensor'), may hold values from -7.5 to 7.5
- pool: bfloat16 [768, 128, 2, 1024], P('replica', None, None, 'tensor'), may hold values from -240 to 240
- page_table: int32 [32, 12], P('replica'), may hold values from 0 to 767, as said below
- hist_len: int32 [32], P('replica'), may hold values from 769 to 1536
- o_weight: bfloat16 [8192, 8192], P('tensor'), may hold values from -0.125 to 0.125
Outputs:
- mixed: bfloat16 [1024, 8192], P(('replica', 'tensor'))
Inputs may be any that keep to these rules, and one draw needn't show every extreme that they name: `page_table`: no two entries are equal. The owner of page id g is the replica group g // 48. Among the live pages (entry j of conversation c with j * 128 < hist_len[c]) of the conversations of one replica group, at most 3 have any one owner, and in every group some owner holds exactly 3 of them.
All inputs are finite; a program needn't handle non-finite values.
Results may differ from a plain program's by a relative error of at most 0.014.
Values may be sent and summed in bfloat16 or wider, within the bound.
No kernel may reach another device: no remote copies, remote signals or barrier semaphores. Data moves between devices by JAX's collectives and lax.ppermute only.
A program may use at most 128 MiB of HBM per device.

v0:
```python
import math

import jax
import jax.numpy as jnp
from jax import lax
from jax.sharding import Mesh
from jax.sharding import PartitionSpec as P

HD = 128
PAGE = 128
SLOT = 3
REPLICA = ("replica_0", "replica_1")
REPLICA_TENSOR = ("replica_0", "replica_1", "tensor")


floor_value = -1e30


def gather_axes(x, axes, dim):
    if not axes:
        return x
    nearer = lax.all_gather(x, axes[-1], axis=dim, tiled=True)
    return gather_axes(nearer, axes[:-1], dim)


def in_blocks(x, dim, devices):
    shape = x.shape
    blocks = x.reshape(*shape[:dim], devices, shape[dim] // devices, *shape[dim + 1 :])
    return jnp.moveaxis(blocks, dim, 0)


def sum_at_owner(x, axis, dim):
    devices = lax.axis_size(axis)
    blocks = lax.all_to_all(in_blocks(x, dim, devices), axis, 0, 0, tiled=True)
    return jnp.sum(blocks.astype(jnp.float32), axis=0)


def attend_part(asked, keys, values, allowed):
    scores = jnp.einsum(
        "bnkgd,btkd->bnkgt", asked, keys, preferred_element_type=jnp.float32
    ) / math.sqrt(HD)
    peak = jnp.max(jnp.where(allowed, scores, floor_value), axis=-1)
    weights = jnp.where(allowed, jnp.exp(scores - peak[..., None]), 0.0).astype(jnp.bfloat16)
    amount = jnp.sum(weights.astype(jnp.float32), axis=-1)
    summed = jnp.einsum("bnkgt,btkd->bnkgd", weights, values, preferred_element_type=jnp.float32)
    return (peak, amount, summed)


def merge(first, second):
    peak = jnp.maximum(first[0], second[0])
    keep = jnp.exp(first[0] - peak)
    take = jnp.exp(second[0] - peak)
    return (
        peak,
        keep * first[1] + take * second[1],
        keep[..., None] * first[2] + take[..., None] * second[2],
    )


def block_stats(asked, pages, dialog_ids, slot_fill):
    dialogs = asked.shape[0]
    slots, page_len = (pages.shape[0], pages.shape[1])
    kv_count = asked.shape[2]
    keys = pages[:, :, 0].reshape(slots, page_len, kv_count, HD)
    values = pages[:, :, 1].reshape(slots, page_len, kv_count, HD)
    belongs = (dialog_ids[:, None] == jnp.arange(dialogs, dtype=jnp.int32)[None, :]) & (
        slot_fill > 0
    )[:, None]
    picker = (dialog_ids[:, None] == jnp.arange(dialogs, dtype=jnp.int32)[None, :]).astype(
        asked.dtype
    )
    chosen = jnp.einsum(
        "sd,dnkgh->snkgh", picker, asked, preferred_element_type=jnp.float32
    ).astype(asked.dtype)
    allowed = (jnp.arange(page_len, dtype=jnp.int32)[None, :] < slot_fill[:, None])[
        :, None, None, None, :
    ]
    peak, amount, summed = attend_part(chosen, keys, values, allowed)
    select = belongs[:, :, None, None, None]
    peaks = jnp.where(select, peak[:, None], floor_value)
    highest = jnp.max(peaks, axis=0)
    factor = jnp.where(select, jnp.exp(peaks - highest[None]), 0.0)
    total = jnp.einsum("sdnkg,snkg->dnkg", factor, amount, precision=lax.Precision.HIGHEST)
    weighted = jnp.einsum("sdnkg,snkgh->dnkgh", factor, summed, precision=lax.Precision.HIGHEST)
    return (highest, total, weighted)


def request_lists(page_table, hist_len, groups, pool_size):
    dialogs, entries = page_table.shape
    position = jnp.arange(entries, dtype=jnp.int32)
    fills = jnp.clip(hist_len[:, None] - position[None, :] * PAGE, 0, PAGE).reshape(-1)
    owners = (page_table // pool_size).reshape(-1)
    shelf = (page_table % pool_size).reshape(-1)
    dialog_of = jnp.repeat(jnp.arange(dialogs, dtype=jnp.int32), entries)
    hits = (owners[:, None] == jnp.arange(groups, dtype=jnp.int32)[None, :]) & (fills > 0)[:, None]
    ranks = jnp.cumsum(hits.astype(jnp.int32), axis=0) - 1
    places = hits.T[:, None, :] & (
        ranks.T[:, None, :] == jnp.arange(SLOT, dtype=jnp.int32)[None, :, None]
    )
    picked = places.astype(jnp.int32)
    wanted = jnp.sum(picked * shelf[None, None, :], axis=-1)
    dialog_ids = jnp.sum(picked * dialog_of[None, None, :], axis=-1)
    slot_fill = jnp.sum(picked * fills[None, None, :], axis=-1)
    return (wanted, dialog_ids, slot_fill)


def local(queries, kv_new, pool, page_table, hist_len, o_weight):
    groups = lax.axis_size(REPLICA)
    pool_size = pool.shape[0]
    dialogs = page_table.shape[0]
    token_rows = queries.shape[0]
    new_len = token_rows // dialogs
    kv_width = kv_new.shape[2]
    kv_count = kv_width // HD
    per_group = queries.shape[1] // kv_width
    asked = queries.reshape(dialogs, new_len, kv_count, per_group, HD)
    fresh = kv_new.reshape(dialogs, new_len, 2, kv_count, HD)
    order = jnp.arange(new_len, dtype=jnp.int32)
    causal = (order[None, :] <= order[:, None])[None, :, None, None, :]
    state = attend_part(asked, fresh[:, :, 0], fresh[:, :, 1], causal)
    wanted, dialog_ids, slot_fill = request_lists(page_table, hist_len, groups, pool_size)
    shelf_ids, their_dialogs, their_fill = (
        lax.all_to_all(wanted, REPLICA, split_axis=0, concat_axis=0, tiled=True),
        lax.all_to_all(dialog_ids, REPLICA, split_axis=0, concat_axis=0, tiled=True),
        lax.all_to_all(slot_fill, REPLICA, split_axis=0, concat_axis=0, tiled=True),
    )
    everyone = gather_axes(queries, REPLICA, 0)
    everyone = everyone.reshape(groups, dialogs, new_len, kv_count, per_group, HD)

    def serve(items):
        shelf_row, reader_dialogs, reader_fill, reader_asked = items
        return block_stats(reader_asked, pool[shelf_row], reader_dialogs, reader_fill)

    partial_value = lax.map(serve, (shelf_ids, their_dialogs, their_fill, everyone))
    returned = (
        lax.all_to_all(partial_value[0], REPLICA, split_axis=0, concat_axis=0, tiled=True),
        lax.all_to_all(partial_value[1], REPLICA, split_axis=0, concat_axis=0, tiled=True),
        lax.all_to_all(partial_value[2], REPLICA, split_axis=0, concat_axis=0, tiled=True),
    )

    def absorb_partial(carry, items):
        return (merge(carry, items), None)

    state, _ = lax.scan(absorb_partial, state, returned)
    attended = (
        (state[2] / state[1][..., None])
        .astype(jnp.bfloat16)
        .reshape(token_rows, kv_count * per_group * HD)
    )
    mixed = sum_at_owner(
        jnp.dot(attended, o_weight, preferred_element_type=jnp.float32).astype(jnp.bfloat16),
        "tensor",
        0,
    )
    return mixed.astype(jnp.bfloat16)


def solution(mesh):
    split = Mesh(
        mesh.devices.reshape(4, 4, mesh.shape["tensor"]), ("replica_0", "replica_1", "tensor")
    )
    in_specs = (
        P(REPLICA, "tensor"),
        P(REPLICA, None, "tensor"),
        P(REPLICA, None, None, "tensor"),
        P(REPLICA, None),
        P(REPLICA),
        P("tensor", None),
    )
    out_specs = P(REPLICA_TENSOR, None)
    return jax.shard_map(local, mesh=split, in_specs=in_specs, out_specs=out_specs, check_vma=False)
```

profile of v0, /device:TPU:68, one launch (start us, length us, event | category | flops | bytes accessed | tf_op | source)
XLA Modules:
  0.0 336.1 jit_solution(9573099112890998430)
XLA Ops:
  6.5 13.7 %all_gather.6 = bf16[256,1024]{1,0:T(8,128)(2,1)} all-gather(bf16[64,1024]{1,0:T(8,128)(2,1)} %param.10), channel_id=1, replica_groups=mesh['replica_0'=4,'replica_1'=4,'tensor'=8] {'replica_1'}, dimensions={0}, use_global_device_ids=true | all-gather | bytes 655360 | tf_op jit(solution)/shard_map/all_gather | solution.py:22
  23.2 7.4 %all-to-all-start = ((s32[16,1,3]{2,1,0:T(1,128)}), s32[16,1,3]{2,1,0:T(1,128)S(1)}, u32[]{:S(2)}, u32[]{:S(2)}) async-start(s32[16,1,3]{2,1,0:T(1,128)} %copy.120), calls=%async_computation | async-start | bytes 16384 | tf_op jit(solution)/shard_map/all_to_all | solution.py:124
  31.3 2.8 all-to-all-done
  34.1 7.5 %all-to-all-start.1 = ((s32[16,1,3]{2,1,0:T(1,128)}), s32[16,1,3]{2,1,0:T(1,128)S(1)}, u32[]{:S(2)}, u32[]{:S(2)}) async-start(s32[16,1,3]{2,1,0:T(1,128)} %copy.122), calls=%async_computation.1 | async-start | bytes 16384 | tf_op jit(solution)/shard_map/all_to_all | solution.py:125
  42.2 4.5 %copy.130 = bf16[48,128,2,128]{3,1,2,0:T(8,128)(2,1)} copy(bf16[48,128,2,128]{3,2,1,0:T(2,128)(2,1)} %param.12) | data formatting | bytes 6291456 | tf_op jit(solution)/shard_map/while | solution.py:134
  46.7 7.2 %all-to-all-start.2 = ((s32[16,1,3]{2,1,0:T(1,128)}), s32[16,1,3]{2,1,0:T(1,128)S(1)}, u32[]{:S(2)}, u32[]{:S(2)}) async-start(s32[16,1,3]{2,1,0:T(1,128)} %copy.124), calls=%async_computation.2 | async-start | bytes 16384 | tf_op jit(solution)/shard_map/all_to_all | solution.py:123
  53.9 2.2 copy.158
  57.4 133.6 %while.30 = (s32[]{:T(128)}, f32[16,2,32,1,8]{2,4,1,3,0:T(8,128)S(1)}, f32[16,2,32,1,8]{2,4,3,1,0:T(8,128)S(1)}, f32[16,2,32,1,8,128]{5,4,2,1,3,0:T(8,128)}, s32...) while((s32[]{:T(128)}, ...), condition=%wide.region_10.11_spmd.clone, body=%wide.region_6.10_spmd.sunk.clone | while | flops 54278048 | bytes 4295727 | solution.py:134
  57.9 2.5 gather_fusion
  62.8 2.2 convolution_bitcast_fusion.8
  66.2 2.5 gather_fusion
  71.2 2.2 convolution_bitcast_fusion.8
  74.6 2.5 gather_fusion
  79.5 2.2 convolution_bitcast_fusion.8
  82.9 2.5 gather_fusion
  87.8 2.2 convolution_bitcast_fusion.8
  91.3 2.5 gather_fusion
  96.2 2.2 convolution_bitcast_fusion.8
  99.6 2.5 gather_fusion
  104.5 2.2 convolution_bitcast_fusion.8
  108.0 2.5 gather_fusion
  112.9 2.2 convolution_bitcast_fusion.8
  116.3 2.5 gather_fusion
  121.2 2.2 convolution_bitcast_fusion.8
  124.7 2.5 gather_fusion
  129.6 2.2 convolution_bitcast_fusion.8
  133.0 2.5 gather_fusion
  138.0 2.2 convolution_bitcast_fusion.8
  141.4 2.5 gather_fusion
  146.3 2.2 convolution_bitcast_fusion.8
  149.7 2.5 gather_fusion
  154.7 2.2 convolution_bitcast_fusion.8
  158.1 2.5 gather_fusion
  163.0 2.2 convolution_bitcast_fusion.8
  166.5 2.5 gather_fusion
  171.4 2.2 convolution_bitcast_fusion.8
  174.8 2.5 gather_fusion
  179.7 2.2 convolution_bitcast_fusion.8
  183.1 2.5 gather_fusion
  188.1 2.2 convolution_bitcast_fusion.8
  191.7 7.5 %all-to-all-start.3 = ((f32[16,1,512]{2,1,0:T(1,128)}), f32[16,1,512]{2,1,0:T(1,128)S(1)}, u32[]{:S(2)}, u32[]{:S(2)}) async-start(f32[16,1,512]{2,1,0:T(1,128)} %reshape.326), calls=%async_computation.3 | async-start | bytes 65536 | tf_op jit(solution)/shard_map/all_to_all | solution.py:136
  199.3 3.6 %all-to-all-done.3 = f32[16,1,512]{2,1,0:T(1,128)S(1)} async-done(((f32[16,1,512]{2,1,0:T(1,128)}), f32[16,1,512]{2,1,0:T(1,128)S(1)}, u32[]{:S(2)}, u32[]{:S(2)}) %all-to-all-start.3) | async-done | bytes 32800 | tf_op jit(solution)/shard_map/all_to_all | solution.py:136
  202.9 10.7 %all_to_all.56 = f32[16,1,512]{2,1,0:T(1,128)S(1)} all-to-all(f32[16,1,512]{2,1,0:T(1,128)S(1)} %reshape.328), channel_id=1, replica_groups=mesh['replica_0'=4,'replica_1'=4,'tensor'=8] {'replica_0','replica_1'}, dimensions={0} | all-to-all | bytes 65536 | tf_op jit(solution)/shard_map/all_to_all | solution.py:137
  213.6 8.5 %all-to-all-start.5 = ((f32[16,2,32,1,8,128]{5,4,2,1,3,0:T(8,128)}), f32[16,2,32,1,8,128]{5,4,2,1,3,0:T(8,128)}, u32[]{:S(2)}, u32[]{:S(2)}) async-start(f32[16,2,32,1,8,128]{5,4,2,1,3,0:T(8,128)} %get-tuple-element.94), calls=%async_computation.5 | async-start | bytes 8388608 | tf_op jit(solution)/shard_map/all_to_all | solution.py:138
  225.1 49.0 %all-to-all-done.5 = f32[16,2,32,1,8,128]{5,4,2,1,3,0:T(8,128)} async-done(((f32[16,2,32,1,8,128]{5,4,2,1,3,0:T(8,128)}), f32[16,2,32,1,8,128]{5,4,2,1,3,0:T(8,128)}, u32[]{:S(2)}, u32[]{:S(2)}) %all-to-all-start.5) | async-done | bytes 4194336 | tf_op jit(solution)/shard_map/all_to_all | solution.py:138
  274.0 23.2 %while.31 = (s32[]{:T(128)}, f32[2,32,1,8]{1,3,2,0:T(8,128)S(1)}, f32[2,32,1,8]{1,3,2,0:T(8,128)S(1)}, f32[2,32,1,8,128]{4,3,2,1,0:T(8,128)S(1)}, f32[16,2,32,1,...) while((s32[]{:T(128)}, f32[2,32,1,8]{1,3,2,0:T(8,128)S(1)}, ...), condition=%wide.region_12.13_spmd.clone, body=%wide.region_11.12_spmd.sunk.clone | while | flops 200194 | bytes 825441 | solution.py:144
  297.5 8.8 %fusion.23 = bf16[8,8,8192]{2,1,0:T(8,128)(2,1)S(1)} fusion(bf16[1024,8192]{1,0:T(8,128)(2,1)} %param.15, bf16[8,8,8,128]{3,2,1,0:T(8,128)(2,1)S(1)} %bitcast.220), kind=kOutput, calls=%fused_computation.55 | convolution fusion | flops 1074266112 | bytes 17956864 | tf_op jit(solution)/shard_map/dot_general | solution.py:151
  306.3 22.1 %all_to_all.57 = bf16[8,8,8192]{2,1,0:T(8,128)(2,1)S(1)} all-to-all(bf16[8,8,8192]{2,1,0:T(8,128)(2,1)S(1)} %fusion.23), channel_id=1, replica_groups=mesh['replica_0'=4,'replica_1'=4,'tensor'=8] {'tensor'}, dimensions={0} | all-to-all | bytes 2097152 | tf_op jit(solution)/shard_map/all_to_all | solution.py:34
  (480 shorter events, 90.5 us)
Async XLA Ops:
  6.5 47.4 %all-gather.2.cloned.1.call-start = ((), (), s32[]{:S(2)}) async-start(), calls=%async_computation.7 | async-start | bytes 2621440 | tf_op jit(solution)/shard_map/all_gather | solution.py:22
  23.2 10.9 %all-to-all-start = ((s32[16,1,3]{2,1,0:T(1,128)}), s32[16,1,3]{2,1,0:T(1,128)S(1)}, u32[]{:S(2)}, u32[]{:S(2)}) async-start(s32[16,1,3]{2,1,0:T(1,128)} %copy.120), calls=%async_computation | async-start | bytes 16384 | tf_op jit(solution)/shard_map/all_to_all | solution.py:124
  34.1 12.6 %all-to-all-start.1 = ((s32[16,1,3]{2,1,0:T(1,128)}), s32[16,1,3]{2,1,0:T(1,128)S(1)}, u32[]{:S(2)}, u32[]{:S(2)}) async-start(s32[16,1,3]{2,1,0:T(1,128)} %copy.122), calls=%async_computation.1 | async-start | bytes 16384 | tf_op jit(solution)/shard_map/all_to_all | solution.py:125
  46.7 10.7 %all-to-all-start.2 = ((s32[16,1,3]{2,1,0:T(1,128)}), s32[16,1,3]{2,1,0:T(1,128)S(1)}, u32[]{:S(2)}, u32[]{:S(2)}) async-start(s32[16,1,3]{2,1,0:T(1,128)} %copy.124), calls=%async_computation.2 | async-start | bytes 16384 | tf_op jit(solution)/shard_map/all_to_all | solution.py:123
  191.7 11.2 %all-to-all-start.3 = ((f32[16,1,512]{2,1,0:T(1,128)}), f32[16,1,512]{2,1,0:T(1,128)S(1)}, u32[]{:S(2)}, u32[]{:S(2)}) async-start(f32[16,1,512]{2,1,0:T(1,128)} %reshape.326), calls=%async_computation.3 | async-start | bytes 65536 | tf_op jit(solution)/shard_map/all_to_all | solution.py:136
  213.6 8.5 %copy-start = (bf16[64,1024]{1,0:T(8,128)(2,1)S(1)}, bf16[64,1024]{1,0:T(8,128)(2,1)}, u32[]{:S(2)}) copy-start(bf16[64,1024]{1,0:T(8,128)(2,1)} %param.10) | copy-start | bytes 393220
  213.6 8.5 %copy-start.1 = (bf16[64,2,128]{2,1,0:T(2,128)(2,1)S(1)}, bf16[64,2,128]{2,1,0:T(2,128)(2,1)}, u32[]{:S(2)}) copy-start(bf16[64,2,128]{2,1,0:T(2,128)(2,1)} %param.11) | copy-start | bytes 98308
  213.6 60.4 %all-to-all-start.5 = ((f32[16,2,32,1,8,128]{5,4,2,1,3,0:T(8,128)}), f32[16,2,32,1,8,128]{5,4,2,1,3,0:T(8,128)}, u32[]{:S(2)}, u32[]{:S(2)}) async-start(f32[16,2,32,1,8,128]{5,4,2,1,3,0:T(8,128)} %get-tuple-element.94), calls=%async_computation.5 | async-start | bytes 8388608 | tf_op jit(solution)/shard_map/all_to_all | solution.py:138
Sparse Core Ops, SparseCore 0:
  20.4 31.2 all-gather.1
where the time goes:
time: 338 us; the launch traced here: 336 us
  local copies, waits for them, and re-layouts  75.7 us (22%)
  matrix products  60.2 us (18%)
  waiting for transfers between devices  56.6 us (17%)
  blocking collectives  46.5 us (14%)
  other arithmetic  43.4 us (13%)
  starting transfers between devices  38.1 us (11%)
  between operations  13.6 us (4%)
    all_to_all x1, waiting for transfers between devices, local(): lax.all_to_all(partial_value[2], REPLICA, split_axis=0, concat_axis=0, ti...  49 us
    gather x16, local copies, waits for them, and re-layouts, serve(): pool[shelf_row]  39.6 us
    dot_general x16, matrix products, block_stats(): jnp.einsum('sdnkg,snkgh->dnkgh', factor, summed, precision=lax.Precision....  35.1 us
    all_to_all x1, blocking collectives, sum_at_owner(): blocks = lax.all_to_all(in_blocks(x, dim, devices), axis, 0, 0, tiled=True)  22.1 us
    add x16, other arithmetic, merge(): keep[..., None] * first[2] + take[..., None] * second[2]  19.6 us
    all_gather x1, blocking collectives, gather_axes(): nearer = lax.all_gather(x, axes[-1], axis=dim, tiled=True)  13.7 us
    dynamic_update_slice x48, local copies, waits for them, and re-layouts, local(): lax.map(serve, (shelf_ids, their_dialogs, their_fill, everyone))  11.9 us
    all_to_all x1, blocking collectives, local(): lax.all_to_all(partial_value[1], REPLICA, split_axis=0, concat_axis=0, ti...  10.7 us
  transfers between devices with their start and end apart: 6, of which 4 were waited for; matrix products, arithmetic and copies ran while one was open for 4% of the time, Pallas kernels for 0%

commit v1 on v0

v1 whole, which is shorter than its diff:
```python
import functools
import math

import jax
import jax.numpy as jnp
from jax import lax
from jax.experimental import pallas as pl
from jax.experimental.pallas import tpu as pltpu
from jax.sharding import Mesh
from jax.sharding import PartitionSpec as P

HD = 128
PAGE = 128
SLOT = 3
LANES = 128
FLOOR = -1e30
REPLICA = ("replica_0", "replica_1")
TENSOR = ("row", "core")


def plan_kernel(groups, pool_size, table, length, wanted, place, count):
    dialogs, entries = table.shape

    def clear(owner, _):
        count[owner] = 0
        for slot in range(SLOT):
            wanted[owner, 0, slot] = 0
        return 0

    lax.fori_loop(0, groups, clear, 0)

    def one(index, _):
        dialog = index // entries
        entry = index % entries
        page = table[dialog, entry]
        owner = page // pool_size
        live = entry * PAGE < length[dialog]
        rank = count[owner]

        @pl.when(live)
        def _():
            wanted[owner, 0, rank] = page - owner * pool_size
            count[owner] = rank + 1

        place[dialog, entry] = jnp.where(live, owner * SLOT + rank, 0)
        return 0

    lax.fori_loop(0, dialogs * entries, one, 0)


def plan(page_table, hist_len, groups, pool_size):
    smem = pl.BlockSpec(memory_space=pltpu.SMEM)
    return pl.pallas_call(
        functools.partial(plan_kernel, groups, pool_size),
        out_shape=(
            jax.ShapeDtypeStruct((groups, 1, LANES), jnp.int32),
            jax.ShapeDtypeStruct(page_table.shape, jnp.int32),
        ),
        in_specs=[smem, smem],
        out_specs=(smem, smem),
        scratch_shapes=[pltpu.SMEM((groups,), jnp.int32)],
        name="plan",
    )(page_table, hist_len)


def collect_kernel(groups, asked, pool, out, held, came, left):
    def arrive(owner, slot):
        return pltpu.make_async_copy(
            pool.at[asked[owner, 0, slot]], held.at[owner, slot], came.at[owner, slot]
        )

    def leave(owner):
        return pltpu.make_async_copy(held.at[owner], out.at[owner], left.at[owner])

    for owner in range(groups):
        for slot in range(SLOT):
            arrive(owner, slot).start()
    for owner in range(groups):
        for slot in range(SLOT):
            arrive(owner, slot).wait()
        leave(owner).start()
    for owner in range(groups):
        leave(owner).wait()


def collect(asked, pool, groups):
    shape = (groups, SLOT) + pool.shape[1:]
    return pl.pallas_call(
        functools.partial(collect_kernel, groups),
        out_shape=jax.ShapeDtypeStruct(shape, pool.dtype),
        in_specs=[
            pl.BlockSpec(memory_space=pltpu.SMEM),
            pl.BlockSpec(memory_space=pl.ANY),
        ],
        out_specs=pl.BlockSpec(memory_space=pl.ANY),
        scratch_shapes=[
            pltpu.VMEM(shape, pool.dtype),
            pltpu.SemaphoreType.DMA((groups, SLOT)),
            pltpu.SemaphoreType.DMA((groups,)),
        ],
        name="collect",
    )(asked, pool)


def attend_kernel(
    tensor_rows,
    place,
    length,
    core,
    queries,
    keys_new,
    values_new,
    pages,
    weight,
    give,
    keep,
    held,
    panel,
    mixed,
    page_sem,
    panel_sem,
):
    dialogs, entries = place.shape
    rows = queries.shape[0]
    fresh = rows // dialogs
    heads = queries.shape[1] // HD
    panels = panel.shape[0]
    width = panel.shape[2]

    def page_copy(dialog, entry):
        return pltpu.make_async_copy(
            pages.at[place[dialog, entry]], held.at[dialog, entry], page_sem.at[dialog, entry]
        )

    def panel_copy(index):
        return pltpu.make_async_copy(
            weight.at[:, pl.ds(index * width, width)], panel.at[index], panel_sem.at[index]
        )

    for dialog in range(dialogs):
        for entry in range(entries):
            page_copy(dialog, entry).start()
    for index in range(panels):
        panel_copy(index).start()

    scale = 1.0 / math.sqrt(HD)
    nt = (((1,), (1,)), ((), ()))
    nn = (((1,), (0,)), ((), ()))
    pieces = []
    for dialog in range(dialogs):
        own = slice(dialog * fresh, (dialog + 1) * fresh)
        asked = jnp.concatenate(
            [queries[own, head * HD : (head + 1) * HD] for head in range(heads)], axis=0
        )
        score_new = (
            lax.dot_general(asked, keys_new[own, :], nt, preferred_element_type=jnp.float32) * scale
        )
        row = lax.broadcasted_iota(jnp.int32, score_new.shape, 0) % fresh
        col = lax.broadcasted_iota(jnp.int32, score_new.shape, 1)
        score_new = jnp.where(col <= row, score_new, FLOOR)
        for entry in range(entries):
            page_copy(dialog, entry).wait()
        keys = held[dialog, :, 0].reshape(entries * PAGE, HD)
        values = held[dialog, :, 1].reshape(entries * PAGE, HD)
        score = lax.dot_general(asked, keys, nt, preferred_element_type=jnp.float32) * scale
        token = lax.broadcasted_iota(jnp.int32, score.shape, 1)
        score = jnp.where(token < length[dialog], score, FLOOR)
        peak = jnp.maximum(
            jnp.max(score, axis=1, keepdims=True), jnp.max(score_new, axis=1, keepdims=True)
        )
        part = jnp.exp(score - peak).astype(jnp.bfloat16)
        part_new = jnp.exp(score_new - peak).astype(jnp.bfloat16)
        amount = jnp.sum(part.astype(jnp.float32), axis=1, keepdims=True) + jnp.sum(
            part_new.astype(jnp.float32), axis=1, keepdims=True
        )
        summed = lax.dot_general(
            part, values, nn, preferred_element_type=jnp.float32
        ) + lax.dot_general(part_new, values_new[own, :], nn, preferred_element_type=jnp.float32)
        attended = summed / amount
        pieces.append(
            jnp.concatenate(
                [attended[head * fresh : (head + 1) * fresh, :] for head in range(heads)], axis=1
            )
        )
    attended = jnp.concatenate(pieces, axis=0)
    block = rows // (2 * tensor_rows)
    sides = [
        jnp.concatenate(
            [
                attended[(2 * index + side) * block : (2 * index + side + 1) * block, :]
                for index in range(tensor_rows)
            ],
            axis=0,
        )
        for side in range(2)
    ]
    first = core[0] == 0
    mixed[...] = jnp.concatenate(
        [jnp.where(first, sides[1], sides[0]), jnp.where(first, sides[0], sides[1])], axis=0
    ).astype(jnp.bfloat16)
    half = rows // 2
    for index in range(panels):
        panel_copy(index).wait()
        product = lax.dot_general(
            mixed[...], panel[index], nn, preferred_element_type=jnp.float32
        ).astype(jnp.bfloat16)
        give[:, index * width : (index + 1) * width] = product[:half]
        keep[:, index * width : (index + 1) * width] = product[half:]


def attend(place, hist_len, core, queries, keys_new, values_new, pages, weight, tensor_rows):
    dialogs, entries = place.shape
    rows = queries.shape[0]
    panels = 8
    out = jax.ShapeDtypeStruct((rows // 2, weight.shape[1]), jnp.bfloat16)
    smem = pl.BlockSpec(memory_space=pltpu.SMEM)
    vmem = pl.BlockSpec(memory_space=pltpu.VMEM)
    hbm = pl.BlockSpec(memory_space=pl.ANY)
    return pl.pallas_call(
        functools.partial(attend_kernel, tensor_rows),
        out_shape=(out, out),
        in_specs=[smem, smem, smem, vmem, vmem, vmem, hbm, hbm],
        out_specs=(vmem, vmem),
        scratch_shapes=[
            pltpu.VMEM((dialogs, entries) + pages.shape[1:], pages.dtype),
            pltpu.VMEM((panels, weight.shape[0], weight.shape[1] // panels), weight.dtype),
            pltpu.VMEM((rows, weight.shape[0]), jnp.bfloat16),
            pltpu.SemaphoreType.DMA((dialogs, entries)),
            pltpu.SemaphoreType.DMA((panels,)),
        ],
        compiler_params=pltpu.CompilerParams(vmem_limit_bytes=48 * 1024 * 1024),
        name="attend",
    )(place, hist_len, core, queries, keys_new, values_new, pages, weight)


def local(queries, kv_new, pool, page_table, hist_len, o_weight):
    groups = lax.axis_size(REPLICA)
    pool_size = pool.shape[0]
    tensor_rows = lax.axis_size("row")
    wanted, place = plan(page_table, hist_len, groups, pool_size)
    asked = lax.all_to_all(wanted, REPLICA, split_axis=0, concat_axis=0, tiled=True)
    shelves = jnp.swapaxes(pool, 1, 2)
    sent = collect(asked, shelves, groups)
    pages = lax.all_to_all(sent, REPLICA, split_axis=0, concat_axis=0, tiled=True)
    pages = pages.reshape((groups * SLOT,) + pages.shape[2:])
    core = lax.axis_index("core").astype(jnp.int32).reshape(1)
    give, keep = attend(
        place, hist_len, core, queries, kv_new[:, 0], kv_new[:, 1], pages, o_weight, tensor_rows
    )
    came = lax.ppermute(give, "core", [(0, 1), (1, 0)])
    pair = (keep.astype(jnp.float32) + came.astype(jnp.float32)).astype(jnp.bfloat16)
    pair = pair.reshape(tensor_rows, -1, pair.shape[1])
    blocks = lax.all_to_all(pair, "row", split_axis=0, concat_axis=0, tiled=True)
    return jnp.sum(blocks.astype(jnp.float32), axis=0).astype(jnp.bfloat16)


def solution(mesh):
    split = Mesh(
        mesh.devices.reshape(4, 4, mesh.shape["tensor"] // 2, 2), REPLICA + TENSOR
    )
    in_specs = (
        P(REPLICA, TENSOR),
        P(REPLICA, None, TENSOR),
        P(REPLICA, None, None, TENSOR),
        P(REPLICA, None),
        P(REPLICA),
        P(TENSOR, None),
    )
    out_specs = P(REPLICA + TENSOR, None)
    return jax.shard_map(local, mesh=split, in_specs=in_specs, out_specs=out_specs, check_vma=False)
```

time: 338 us -> 98 us (0.29)
  the two profiles are of different devices: /device:TPU:68 before, /device:TPU:0 now
where the time goes in v1:
time: 98 us; the launch traced here: 97.7 us
  waiting for transfers between devices  47.6 us (49%)
  Pallas kernels  17.9 us (18%)
  blocking collectives  14 us (14%)
  starting transfers between devices  12.1 us (12%)
  local copies, waits for them, and re-layouts  5.04 us (5%)
    all_to_all x1, waiting for transfers between devices, local(): lax.all_to_all(sent, REPLICA, split_axis=0, concat_axis=0, tiled=True)  42.6 us
    all_to_all x1, blocking collectives, local(): lax.all_to_all(pair, 'row', split_axis=0, concat_axis=0, tiled=True)  14 us
    pallas_call x1, Pallas kernels, attend(): pl.pallas_call(functools.partial(attend_kernel, tensor_rows), out_shape=(...  9.35 us
    all_to_all x1, starting transfers between devices, local(): lax.all_to_all(wanted, REPLICA, split_axis=0, concat_axis=0, tiled=True)  8 us
    pallas_call x1, Pallas kernels, collect(): pl.pallas_call(functools.partial(collect_kernel, groups), out_shape=jax.S...  6.23 us
    unnamed x11, local copies, waits for them, and re-layouts  4.98 us
    all_to_all x1, starting transfers between devices, local(): lax.all_to_all(sent, REPLICA, split_axis=0, concat_axis=0, tiled=True)  4.01 us
    all_to_all x1, waiting for transfers between devices, local(): lax.all_to_all(wanted, REPLICA, split_axis=0, concat_axis=0, tiled=True)  3.15 us
  transfers between devices with their start and end apart: 3, of which 3 were waited for; matrix products, arithmetic and copies ran while one was open for 5% of the time, Pallas kernels for 0%

profile of v1, /device:TPU:0, one launch (start us, length us, event | category | flops | bytes accessed | tf_op | source)
XLA Modules:
  0.0 97.7 jit_solution(17334640655240727022)
XLA Ops:
  0.0 2.3 %plan.1 = (s32[16,1,128]{2,1,0:T(1,128)}, s32[2,12]{1,0:T(2,128)}) custom-call(s32[2,12]{1,0:T(2,128)} %table.1, s32[2]{0:T(128)} %length.3), custom_call_target="tpu_custom_call" | custom-call | tf_op jit(solution)/shard_map/plan/pallas_call | solution.py:53
  2.3 8.0 %all-to-all-start = ((s32[16,1,128]{2,1,0:T(1,128)}), s32[16,1,128]{2,1,0:T(1,128)S(1)}, u32[]{:S(2)}, u32[]{:S(2)}) async-start(s32[16,1,128]{2,1,0:T(1,128)} %get-tuple-element.10), calls=%async_computation | async-start | bytes 16384 | tf_op jit(solution)/shard_map/all_to_all | solution.py:241
  10.4 4.4 %copy.15 = bf16[48,128,2,128]{3,1,2,0:T(8,128)(2,1)} copy(bf16[48,128,2,128]{3,2,1,0:T(2,128)(2,1)} %param.8) | data formatting | bytes 6291456 | tf_op args[2]
  14.7 3.2 %all-to-all-done.asked = s32[16,1,128]{2,1,0:T(1,128)S(1)} async-done(((s32[16,1,128]{2,1,0:T(1,128)}), s32[16,1,128]{2,1,0:T(1,128)S(1)}, u32[]{:S(2)}, u32[]{:S(2)}) %all-to-all-start) | async-done | bytes 8224 | tf_op jit(solution)/shard_map/all_to_all | solution.py:241
  17.9 0.0 copy-start.4
  17.9 0.6 copy-done.4
  18.5 6.2 %collect.1 = bf16[16,3,2,128,128]{4,3,2,1,0:T(8,128)(2,1)} custom-call(s32[16,1,128]{2,1,0:T(1,128)} %copy-done.4, bf16[48,2,128,128]{3,2,1,0:T(8,128)(2,1)} %bitcast.12), custom_call_target="tpu_custom_call" | custom-call | tf_op jit(solution)/shard_map/collect/pallas_call | solution.py:88
  24.7 0.0 copy-start.3
  24.7 0.0 copy-start
  24.7 0.0 copy-start.1
  24.7 0.0 copy-start.2
  24.7 4.0 %all-to-all-start.1 = ((bf16[16,3,2,128,128]{4,3,2,1,0:T(8,128)(2,1)}), bf16[16,3,2,128,128]{4,3,2,1,0:T(8,128)(2,1)S(1)}, u32[]{:S(2)}, u32[]{:S(2)}) async-start(bf16[16,3,2,128,128]{4,3,2,1,0:T(8,128)(2,1)} %collect.1), calls=%async_computation.1 | async-start | bytes 6291456 | tf_op jit(solution)/shard_map/all_to_all | solution.py:244
  28.8 0.0 copy-done.3
  28.8 0.1 fusion.1
  28.9 42.6 %all-to-all-done.1 = bf16[16,3,2,128,128]{4,3,2,1,0:T(8,128)(2,1)S(1)} async-done(((bf16[16,3,2,128,128]{4,3,2,1,0:T(8,128)(2,1)}), bf16[16,3,2,128,128]{4,3,2,1,0:T(8,128)(2,1)S(1)}, u32[]{:S(2)}, u32[]{:S(2)}) %all-to-all-start.1) | async-done | bytes 3145760 | tf_op jit(solution)/shard_map/all_to_all | solution.py:244
  71.4 0.0 copy-done
  71.4 0.0 copy-done.1
  71.4 0.0 copy-done.2
  71.4 9.3 %attend.1 = (bf16[32,8192]{1,0:T(8,128)(2,1)S(1)}, bf16[32,8192]{1,0:T(8,128)(2,1)S(1)}) custom-call(s32[2,12]{1,0:T(2,128)S(1)} %copy-done.1, s32[2]{0:T(128)S(1)} %copy-done.2, s32[1]{0:T(128)} %bitcast.core, bf16[64,1024]{1,0:T(8,128)(2,1)S(1)} %copy-done, bf16[64,128]{1,0:T(8,128)(2,1)S(1)} %get-tuple-element.16.keys_new, ...), custom_call_target="tpu_custom_call" | custom-call | tf_op jit(solution)/shard_map/attend/pallas_call | solution.py:219
  80.8 0.1 collective-permute-start
  80.9 1.9 %collective-permute-done = bf16[32,8192]{1,0:T(8,128)(2,1)S(1)} collective-permute-done((bf16[32,8192]{1,0:T(8,128)(2,1)S(1)}, bf16[32,8192]{1,0:T(8,128)(2,1)S(1)}, u32[]{:S(2)}, u32[]{:S(2)}) %collective-permute-start) | collective-permute-done | bytes 524320 | tf_op jit(solution)/shard_map/ppermute | solution.py:250
  82.8 0.1 fusion
  82.9 14.0 %all_to_all.15 = bf16[4,8,8192]{2,1,0:T(8,128)(2,1)S(1)} all-to-all(bf16[4,8,8192]{2,1,0:T(8,128)(2,1)S(1)} %fusion), channel_id=1, replica_groups=mesh['replica_0'=4,'replica_1'=4,'row'=4,'core'=2] {'row'}, dimensions={0} | all-to-all | bytes 1048576 | tf_op jit(solution)/shard_map/all_to_all | solution.py:253
  96.9 0.7 reduce_sum.12
  (1 shorter events, 0.0 us)
Async XLA Ops:
  2.3 15.5 %all-to-all-start = ((s32[16,1,128]{2,1,0:T(1,128)}), s32[16,1,128]{2,1,0:T(1,128)S(1)}, u32[]{:S(2)}, u32[]{:S(2)}) async-start(s32[16,1,128]{2,1,0:T(1,128)} %get-tuple-element.10), calls=%async_computation | async-start | bytes 16384 | tf_op jit(solution)/shard_map/all_to_all | solution.py:241
  17.9 0.6 copy-start.4
  24.7 4.1 %copy-start.3 = (bf16[64,2,128]{2,1,0:T(2,128)(2,1)S(1)}, bf16[64,2,128]{2,1,0:T(2,128)(2,1)}, u32[]{:S(2)}) copy-start(bf16[64,2,128]{2,1,0:T(2,128)(2,1)} %param.7) | copy-start | bytes 98308
  24.7 46.7 %copy-start = (bf16[64,1024]{1,0:T(8,128)(2,1)S(1)}, bf16[64,1024]{1,0:T(8,128)(2,1)}, u32[]{:S(2)}) copy-start(bf16[64,1024]{1,0:T(8,128)(2,1)} %queries.1) | copy-start | bytes 393220
  24.7 46.7 %copy-start.1 = (s32[2,12]{1,0:T(2,128)S(1)}, s32[2,12]{1,0:T(2,128)}, u32[]{:S(2)}) copy-start(s32[2,12]{1,0:T(2,128)} %get-tuple-element.9.place) | copy-start | bytes 292
  24.7 46.7 %copy-start.2 = (s32[2]{0:T(128)S(1)}, s32[2]{0:T(128)}, u32[]{:S(2)}) copy-start(s32[2]{0:T(128)} %length.3) | copy-start | bytes 28
  24.7 46.7 %all-to-all-start.1 = ((bf16[16,3,2,128,128]{4,3,2,1,0:T(8,128)(2,1)}), bf16[16,3,2,128,128]{4,3,2,1,0:T(8,128)(2,1)S(1)}, u32[]{:S(2)}, u32[]{:S(2)}) async-start(bf16[16,3,2,128,128]{4,3,2,1,0:T(8,128)(2,1)} %collect.1), calls=%async_computation.1 | async-start | bytes 6291456 | tf_op jit(solution)/shard_map/all_to_all | solution.py:244
  80.8 2.0 %collective-permute-start = (bf16[32,8192]{1,0:T(8,128)(2,1)S(1)}, bf16[32,8192]{1,0:T(8,128)(2,1)S(1)}, u32[]{:S(2)}, u32[]{:S(2)}) collective-permute-start(bf16[32,8192]{1,0:T(8,128)(2,1)S(1)} %get-tuple-element.12), channel_id=1, source_target_pairs={{0,1},{1,0},{2,3},{3,2},{4,5},{5,4},{6,7},{7,6},{8,9},{9,8},{10,11... | collective-permute-start | bytes 1572872 | tf_op jit(solution)/shard_map/ppermute | solution.py:250

commit v2 on v1

v2 whole, which is shorter than its diff:
```python
import functools
import math

import jax
import jax.numpy as jnp
from jax import lax
from jax.experimental import pallas as pl
from jax.experimental.pallas import tpu as pltpu
from jax.sharding import Mesh
from jax.sharding import PartitionSpec as P

HD = 128
PAGE = 128
SLOT = 3
LANES = 128
FLOOR = -1e30
REPLICA = ("replica_0", "replica_1")
TENSOR = ("row", "core")


def plan_kernel(groups, table, length, pool, wanted, place, near, count, near_sem):
    bring = pltpu.make_async_copy(pool, near, near_sem)
    bring.start()
    dialogs, entries = table.shape
    pool_size = pool.shape[0]
    for owner in range(groups):
        count[owner] = 0
        for slot in range(SLOT):
            wanted[owner, 0, slot] = 0
    for dialog in range(dialogs):
        tokens = length[dialog]
        for entry in range(entries):
            page = table[dialog, entry]
            owner = lax.div(page, pool_size)
            live = entry * PAGE < tokens
            rank = count[owner]

            @pl.when(live)
            def _():
                wanted[owner, 0, rank] = page - owner * pool_size
                count[owner] = rank + 1

            place[dialog, entry] = jnp.where(live, owner * SLOT + rank, 0)
    bring.wait()


def plan(page_table, hist_len, pool, groups):
    smem = pl.BlockSpec(memory_space=pltpu.SMEM)
    return pl.pallas_call(
        functools.partial(plan_kernel, groups),
        out_shape=(
            jax.ShapeDtypeStruct((groups, 1, LANES), jnp.int32),
            jax.ShapeDtypeStruct(page_table.shape, jnp.int32),
            jax.ShapeDtypeStruct(pool.shape, pool.dtype),
        ),
        in_specs=[smem, smem, pl.BlockSpec(memory_space=pltpu.HBM)],
        out_specs=(smem, smem, pl.BlockSpec(memory_space=pltpu.VMEM)),
        scratch_shapes=[pltpu.SMEM((groups,), jnp.int32), pltpu.SemaphoreType.DMA],
        compiler_params=pltpu.CompilerParams(vmem_limit_bytes=50 * 1024 * 1024),
        name="plan",
    )(page_table, hist_len, pool)


def collect_kernel(groups, asked, pool, out, ids, ids_sem):
    read = pltpu.make_async_copy(asked, ids, ids_sem)
    read.start()
    read.wait()
    for owner in range(groups):
        for slot in range(SLOT):
            out[owner, slot] = pool[ids[owner, 0, slot]]


def collect(asked, pool, groups):
    shape = (groups, SLOT) + pool.shape[1:]
    vmem = pl.BlockSpec(memory_space=pltpu.VMEM)
    return pl.pallas_call(
        functools.partial(collect_kernel, groups),
        out_shape=jax.ShapeDtypeStruct(shape, pool.dtype),
        in_specs=[pl.BlockSpec(memory_space=pl.ANY), vmem],
        out_specs=vmem,
        scratch_shapes=[pltpu.SMEM(asked.shape, jnp.int32), pltpu.SemaphoreType.DMA],
        compiler_params=pltpu.CompilerParams(vmem_limit_bytes=8 * 1024 * 1024),
        name="collect",
    )(asked, pool)


def attend_kernel(
    tensor_rows,
    place,
    length,
    queries,
    kv_new,
    pages,
    weight,
    give,
    keep,
    wide,
    wide_new,
    keys,
    values,
    mixed,
    panel,
    panel_sem,
):
    dialogs, entries = place.shape
    rows = queries.shape[0]
    fresh = rows // dialogs
    heads = queries.shape[1] // HD
    panels = panel.shape[0]
    width = panel.shape[2]

    def panel_copy(index):
        return pltpu.make_async_copy(
            weight.at[:, pl.ds(index * width, width)], panel.at[index], panel_sem.at[index]
        )

    for index in range(panels):
        panel_copy(index).start()

    scale = 1.0 / math.sqrt(HD)
    nt = (((1,), (1,)), ((), ()))
    nn = (((1,), (0,)), ((), ()))
    wide_new[...] = kv_new[...].astype(jnp.float32)
    for dialog in range(dialogs):
        for entry in range(entries):
            wide[dialog, entry] = pages[place[dialog, entry]].astype(jnp.float32)
            span = slice(entry * PAGE, (entry + 1) * PAGE)
            keys[dialog, span, :] = wide[dialog, entry, pl.ds(0, PAGE, stride=2), :].astype(
                jnp.bfloat16
            )
            values[dialog, span, :] = wide[dialog, entry, pl.ds(1, PAGE, stride=2), :].astype(
                jnp.bfloat16
            )
    pieces = []
    for dialog in range(dialogs):
        own = slice(dialog * fresh, (dialog + 1) * fresh)
        asked = jnp.concatenate(
            [queries[own, head * HD : (head + 1) * HD] for head in range(heads)], axis=0
        )
        start = dialog * 2 * fresh
        keys_new = wide_new[pl.ds(start, fresh, stride=2), :].astype(jnp.bfloat16)
        values_new = wide_new[pl.ds(start + 1, fresh, stride=2), :].astype(jnp.bfloat16)
        score_new = (
            lax.dot_general(asked, keys_new, nt, preferred_element_type=jnp.float32) * scale
        )
        row = lax.broadcasted_iota(jnp.int32, score_new.shape, 0) % fresh
        col = lax.broadcasted_iota(jnp.int32, score_new.shape, 1)
        score_new = jnp.where(col <= row, score_new, FLOOR)
        score = lax.dot_general(asked, keys[dialog], nt, preferred_element_type=jnp.float32) * scale
        token = lax.broadcasted_iota(jnp.int32, score.shape, 1)
        score = jnp.where(token < length[dialog], score, FLOOR)
        peak = jnp.maximum(
            jnp.max(score, axis=1, keepdims=True), jnp.max(score_new, axis=1, keepdims=True)
        )
        part = jnp.exp(score - peak).astype(jnp.bfloat16)
        part_new = jnp.exp(score_new - peak).astype(jnp.bfloat16)
        amount = jnp.sum(part.astype(jnp.float32), axis=1, keepdims=True) + jnp.sum(
            part_new.astype(jnp.float32), axis=1, keepdims=True
        )
        summed = lax.dot_general(
            part, values[dialog], nn, preferred_element_type=jnp.float32
        ) + lax.dot_general(part_new, values_new, nn, preferred_element_type=jnp.float32)
        attended = summed / amount
        pieces.append(
            jnp.concatenate(
                [attended[head * fresh : (head + 1) * fresh, :] for head in range(heads)], axis=1
            )
        )
    attended = jnp.concatenate(pieces, axis=0)
    block = rows // (2 * tensor_rows)
    sides = [
        jnp.concatenate(
            [
                attended[(2 * index + side) * block : (2 * index + side + 1) * block, :]
                for index in range(tensor_rows)
            ],
            axis=0,
        )
        for side in range(2)
    ]
    first = lax.axis_index("core") == 0
    mixed[...] = jnp.concatenate(
        [jnp.where(first, sides[1], sides[0]), jnp.where(first, sides[0], sides[1])], axis=0
    ).astype(jnp.bfloat16)
    half = rows // 2
    for index in range(panels):
        span = slice(index * width, (index + 1) * width)
        panel_copy(index).wait()
        product = lax.dot_general(
            mixed[...], panel[index], nn, preferred_element_type=jnp.float32
        ).astype(jnp.bfloat16)
        give[:, span] = product[:half]
        keep[:, span] = product[half:]


def attend(place, hist_len, queries, kv_new, pages, weight, tensor_rows):
    dialogs, entries = place.shape
    rows = queries.shape[0]
    out = jax.ShapeDtypeStruct((rows // 2, weight.shape[1]), jnp.bfloat16)
    smem = pl.BlockSpec(memory_space=pltpu.SMEM)
    vmem = pl.BlockSpec(memory_space=pltpu.VMEM)
    panels = 8
    history = (dialogs, entries * PAGE, HD)
    return pl.pallas_call(
        functools.partial(attend_kernel, tensor_rows),
        out_shape=(out, out),
        in_specs=[smem, smem, vmem, vmem, vmem, pl.BlockSpec(memory_space=pltpu.HBM)],
        out_specs=(vmem, vmem),
        scratch_shapes=[
            pltpu.VMEM((dialogs, entries) + pages.shape[1:], jnp.float32),
            pltpu.VMEM(kv_new.shape, jnp.float32),
            pltpu.VMEM(history, jnp.bfloat16),
            pltpu.VMEM(history, jnp.bfloat16),
            pltpu.VMEM((rows, weight.shape[0]), jnp.bfloat16),
            pltpu.VMEM((panels, weight.shape[0], weight.shape[1] // panels), weight.dtype),
            pltpu.SemaphoreType.DMA((panels,)),
        ],
        compiler_params=pltpu.CompilerParams(vmem_limit_bytes=48 * 1024 * 1024),
        name="attend",
    )(place, hist_len, queries, kv_new, pages, weight)


def local(queries, kv_new, pool, page_table, hist_len, o_weight):
    groups = lax.axis_size(REPLICA)
    tensor_rows = lax.axis_size("row")
    shelves = pool.reshape(pool.shape[0], 2 * PAGE, HD)
    wanted, place, shelves = plan(page_table, hist_len, shelves, groups)
    asked = lax.all_to_all(wanted, REPLICA, split_axis=0, concat_axis=0, tiled=True)
    sent = collect(asked, shelves, groups)
    pages = lax.all_to_all(sent, REPLICA, split_axis=0, concat_axis=0, tiled=True)
    pages = pages.reshape(groups * SLOT, 2 * PAGE, HD)
    fresh = kv_new.reshape(2 * kv_new.shape[0], HD)
    give, keep = attend(place, hist_len, queries, fresh, pages, o_weight, tensor_rows)
    came = lax.ppermute(give, "core", [(0, 1), (1, 0)])
    pair = (keep.astype(jnp.float32) + came.astype(jnp.float32)).astype(jnp.bfloat16)
    pair = pair.reshape(tensor_rows, -1, pair.shape[1])
    blocks = lax.all_to_all(pair, "row", split_axis=0, concat_axis=0, tiled=True)
    return jnp.sum(blocks.astype(jnp.float32), axis=0).astype(jnp.bfloat16)


def solution(mesh):
    split = Mesh(
        mesh.devices.reshape(4, 4, mesh.shape["tensor"] // 2, 2), REPLICA + TENSOR
    )
    in_specs = (
        P(REPLICA, TENSOR),
        P(REPLICA, None, TENSOR),
        P(REPLICA, None, None, TENSOR),
        P(REPLICA, None),
        P(REPLICA),
        P(TENSOR, None),
    )
    out_specs = P(REPLICA + TENSOR, None)
    return jax.shard_map(local, mesh=split, in_specs=in_specs, out_specs=out_specs, check_vma=False)
```

time: 98 us -> 87.3 us (0.89)
  blocking collectives: 14 us -> 70.5 us
  waiting for transfers between devices: 47.6 us -> 1.9 us
  starting transfers between devices: 12.1 us -> 0.09 us
  Pallas kernels: 17.9 us -> 12.2 us
  local copies, waits for them, and re-layouts: 5.04 us -> 1.35 us
    all_to_all x0 -> x2, blocking collectives: none -> 56.5 us  [the longest x1 41.1 us: local(): lax.all_to_all(sent, REPLICA, split_axis=0, concat_axis=0, tiled=True)]
    all_to_all x2 -> x0, waiting for transfers between devices: 45.7 us -> none  [the longest x1 42.6 us: local(): lax.all_to_all(sent, REPLICA, split_axis=0, concat_axis=0, tiled=True)]
    all_to_all x2 -> x0, starting transfers between devices: 12 us -> none  [the longest x1 8 us: local(): lax.all_to_all(wanted, REPLICA, split_axis=0, concat_axis=0, tiled=True)]
    pallas_call x1, Pallas kernels: 6.23 us -> 0.88 us  [collect(): pl.pallas_call(functools.partial(collect_kernel, groups), out_shape=jax.S...]
    unnamed x11 -> x10, local copies, waits for them, and re-layouts: 4.98 us -> 1.35 us
    pallas_call x1, Pallas kernels: 9.35 us -> 8.18 us  [attend(): pl.pallas_call(functools.partial(attend_kernel, tensor_rows), out_shape=(...]
  transfers between devices with their start and end apart: 3 -> 1, of which waited for: 3 -> 1; matrix products, arithmetic and copies ran while one was open for 5% -> 0% of each run, Pallas kernels for 0% -> 0%
where the time goes in v2:
time: 87.3 us; the launch traced here: 87.1 us
  blocking collectives  70.5 us (81%)
  Pallas kernels  12.2 us (14%)
  waiting for transfers between devices  1.9 us (2%)
  local copies, waits for them, and re-layouts  1.35 us (2%)
    all_to_all x1, blocking collectives, local(): lax.all_to_all(sent, REPLICA, split_axis=0, concat_axis=0, tiled=True)  41.1 us
    all_to_all x1, blocking collectives, local(): lax.all_to_all(wanted, REPLICA, split_axis=0, concat_axis=0, tiled=True)  15.4 us
    all_to_all x1, blocking collectives, local(): lax.all_to_all(pair, 'row', split_axis=0, concat_axis=0, tiled=True)  14 us
    pallas_call x1, Pallas kernels, attend(): pl.pallas_call(functools.partial(attend_kernel, tensor_rows), out_shape=(...  8.18 us
    pallas_call x1, Pallas kernels, plan(): pl.pallas_call(functools.partial(plan_kernel, groups), out_shape=(jax.Sha...  3.18 us
    ppermute x1, waiting for transfers between devices, local(): came = lax.ppermute(give, 'core', [(0, 1), (1, 0)])  1.9 us
  transfers between devices with their start and end apart: 1, of which 1 were waited for; matrix products, arithmetic and copies ran while one was open for 0% of the time, Pallas kernels for 0%

profile of v2, /device:TPU:0, one launch (start us, length us, event | category | flops | bytes accessed | tf_op | source)
XLA Modules:
  0.0 87.1 jit_solution(10103886972116045475)
XLA Ops:
  0.0 0.0 copy-start.2
  0.0 0.7 copy-done.2
  0.7 0.0 copy-start.4
  0.7 0.7 copy-done.4
  1.3 3.2 %plan.1 = (s32[16,1,128]{2,1,0:T(1,128)S(1)}, s32[2,12]{1,0:T(2,128)S(1)}, bf16[48,256,128]{2,1,0:T(8,128)(2,1)S(1)}) custom-call(s32[2,12]{1,0:T(2,128)S(1)} %copy-done.4, s32[2]{0:T(128)S(1)} %copy-done.2, bf16[48,256,128]{2,1,0:T(8,128)(2,1)} %bitcast.7), custom_call_target="tpu_custom_call" | custom-call | tf_op jit(solution)/shard_map/plan/pallas_call | solution.py:49
  4.5 15.4 %all_to_all.15.asked = s32[16,1,128]{2,1,0:T(1,128)S(1)} all-to-all(s32[16,1,128]{2,1,0:T(1,128)S(1)} %get-tuple-element.11), channel_id=1, replica_groups=mesh['replica_0'=4,'replica_1'=4,'row'=4,'core'=2] {'replica_0','replica..., dimensions={0} | all-to-all | bytes 16384 | tf_op jit(solution)/shard_map/all_to_all | solution.py:228
  19.9 0.9 %collect.1 = bf16[16,3,256,128]{3,2,1,0:T(8,128)(2,1)S(1)} custom-call(s32[16,1,128]{2,1,0:T(1,128)S(1)} %all_to_all.15.asked, bf16[48,256,128]{2,1,0:T(8,128)(2,1)S(1)} %get-tuple-element.12.pool), custom_call_target="tpu_custom_call" | custom-call | tf_op jit(solution)/shard_map/collect/pallas_call | solution.py:76
  20.8 0.0 copy-start
  20.8 0.0 copy-start.1
  20.8 0.0 copy-start.3
  20.8 41.1 %all_to_all.16 = bf16[16,3,256,128]{3,2,1,0:T(8,128)(2,1)S(1)} all-to-all(bf16[16,3,256,128]{3,2,1,0:T(8,128)(2,1)S(1)} %collect.1), channel_id=1, replica_groups=mesh['replica_0'=4,'replica_1'=4,'row'=4,'core'=2] {'replica_0','replica..., dimensions={0} | all-to-all | bytes 6291456 | tf_op jit(solution)/shard_map/all_to_all | solution.py:230
  62.0 0.0 copy-done
  62.0 0.0 copy-done.1
  62.0 0.0 copy-done.3
  62.0 8.2 %attend.1 = (bf16[32,8192]{1,0:T(8,128)(2,1)S(1)}, bf16[32,8192]{1,0:T(8,128)(2,1)S(1)}) custom-call(s32[2,12]{1,0:T(2,128)S(1)} %get-tuple-element.10.place, s32[2]{0:T(128)S(1)} %copy-done.3, bf16[64,1024]{1,0:T(8,128)(2,1)S(1)} %copy-done, bf16[128,128]{1,0:T(8,128)(2,1)S(1)} %bitcast.6, bf16[48,256,128]{2,1,0:T(8,128)(2,1)S(1)} %bitcast.5, ...), custom_call_target="tpu_custom_call" | custom-call | tf_op jit(solution)/shard_map/attend/pallas_call | solution.py:204
  70.2 0.1 collective-permute-start
  70.3 1.9 %collective-permute-done = bf16[32,8192]{1,0:T(8,128)(2,1)S(1)} collective-permute-done((bf16[32,8192]{1,0:T(8,128)(2,1)S(1)}, bf16[32,8192]{1,0:T(8,128)(2,1)S(1)}, u32[]{:S(2)}, u32[]{:S(2)}) %collective-permute-start) | collective-permute-done | bytes 524320 | tf_op jit(solution)/shard_map/ppermute | solution.py:234
  72.2 0.1 fusion
  72.3 14.0 %all_to_all.17 = bf16[4,8,8192]{2,1,0:T(8,128)(2,1)S(1)} all-to-all(bf16[4,8,8192]{2,1,0:T(8,128)(2,1)S(1)} %fusion), channel_id=1, replica_groups=mesh['replica_0'=4,'replica_1'=4,'row'=4,'core'=2] {'row'}, dimensions={0} | all-to-all | bytes 1048576 | tf_op jit(solution)/shard_map/all_to_all | solution.py:237
  86.3 0.7 reduce_sum.12
Async XLA Ops:
  0.0 0.7 copy-start.2
  0.7 0.7 copy-start.4
  20.8 41.2 %copy-start = (bf16[64,1024]{1,0:T(8,128)(2,1)S(1)}, bf16[64,1024]{1,0:T(8,128)(2,1)}, u32[]{:S(2)}) copy-start(bf16[64,1024]{1,0:T(8,128)(2,1)} %queries.1) | copy-start | bytes 393220
  20.8 41.2 %copy-start.1 = (bf16[64,2,128]{2,1,0:T(2,128)(2,1)S(1)}, bf16[64,2,128]{2,1,0:T(2,128)(2,1)}, u32[]{:S(2)}) copy-start(bf16[64,2,128]{2,1,0:T(2,128)(2,1)} %param.7) | copy-start | bytes 98308
  20.8 41.1 %copy-start.3 = (s32[2]{0:T(128)S(1)}, s32[2]{0:T(128)}, u32[]{:S(2)}) copy-start(s32[2]{0:T(128)} %length.3) | copy-start | bytes 28
  70.2 2.0 %collective-permute-start = (bf16[32,8192]{1,0:T(8,128)(2,1)S(1)}, bf16[32,8192]{1,0:T(8,128)(2,1)S(1)}, u32[]{:S(2)}, u32[]{:S(2)}) collective-permute-start(bf16[32,8192]{1,0:T(8,128)(2,1)S(1)} %get-tuple-element.14), channel_id=1, source_target_pairs={{0,1},{1,0},{2,3},{3,2},{4,5},{5,4},{6,7},{7,6},{8,9},{9,8},{10,11... | collective-permute-start | bytes 1572872 | tf_op jit(solution)/shard_map/ppermute | solution.py:234

commit v3 on v2

--- a/solution.py
+++ b/solution.py
@@ -13,6 +13,7 @@
 PAGE = 128
 SLOT = 3
 LANES = 128
+PANELS = 8
 FLOOR = -1e30
 REPLICA = ("replica_0", "replica_1")
 TENSOR = ("row", "core")
@@ -98,7 +99,7 @@
     wide_new,
     keys,
     values,
-    mixed,
+    blocks,
     panel,
     panel_sem,
 ):
@@ -106,8 +107,8 @@
     rows = queries.shape[0]
     fresh = rows // dialogs
     heads = queries.shape[1] // HD
-    panels = panel.shape[0]
-    width = panel.shape[2]
+    block = rows // (2 * tensor_rows)
+    panels, _, width = panel.shape
 
     def panel_copy(index):
         return pltpu.make_async_copy(
@@ -161,63 +162,87 @@
             part, values[dialog], nn, preferred_element_type=jnp.float32
         ) + lax.dot_general(part_new, values_new, nn, preferred_element_type=jnp.float32)
         attended = summed / amount
-        pieces.append(
-            jnp.concatenate(
-                [attended[head * fresh : (head + 1) * fresh, :] for head in range(heads)], axis=1
-            )
-        )
-    attended = jnp.concatenate(pieces, axis=0)
-    block = rows // (2 * tensor_rows)
-    sides = [
-        jnp.concatenate(
-            [
-                attended[(2 * index + side) * block : (2 * index + side + 1) * block, :]
-                for index in range(tensor_rows)
-            ],
+        for head in range(heads):
+            for index in range(fresh // block):
+                first = head * fresh + index * block
+                blocks[dialog * (fresh // block) + index, :, head * HD : (head + 1) * HD] = (
+                    attended[first : first + block, :]
+                )
+    row, core = lax.axis_index("row"), lax.axis_index("core")
+    across, beside = tensor_rows - 1 - row, row ^ 1
+    orders = (
+        (row, across, beside, across ^ 1),
+        (row, beside, across, across ^ 1),
+    )
+    half = rows // 2
+    sides = weight.shape[1] // len(orders)
+    for side, order in enumerate(orders):
+        mixed = jnp.concatenate(
+            [blocks[2 * there + 1 - core] for there in order]
+            + [blocks[2 * there + core] for there in order],
             axis=0,
-        )
-        for side in range(2)
-    ]
-    first = lax.axis_index("core") == 0
-    mixed[...] = jnp.concatenate(
-        [jnp.where(first, sides[1], sides[0]), jnp.where(first, sides[0], sides[1])], axis=0
-    ).astype(jnp.bfloat16)
-    half = rows // 2
-    for index in range(panels):
-        span = slice(index * width, (index + 1) * width)
-        panel_copy(index).wait()
-        product = lax.dot_general(
-            mixed[...], panel[index], nn, preferred_element_type=jnp.float32
         ).astype(jnp.bfloat16)
-        give[:, span] = product[:half]
-        keep[:, span] = product[half:]
+        for index in range(sides // width):
+            number = side * (sides // width) + index
+            span = slice(index * width, (index + 1) * width)
+            panel_copy(number).wait()
+            product = lax.dot_general(
+                mixed, panel[number], nn, preferred_element_type=jnp.float32
+            ).astype(jnp.bfloat16)
+            give[side, :, span] = product[:half]
+            keep[side, :, span] = product[half:]
 
 
 def attend(place, hist_len, queries, kv_new, pages, weight, tensor_rows):
     dialogs, entries = place.shape
     rows = queries.shape[0]
-    out = jax.ShapeDtypeStruct((rows // 2, weight.shape[1]), jnp.bfloat16)
+    out = jax.ShapeDtypeStruct((2, rows // 2, weight.shape[1] // 2), jnp.bfloat16)
     smem = pl.BlockSpec(memory_space=pltpu.SMEM)
     vmem = pl.BlockSpec(memory_space=pltpu.VMEM)
-    panels = 8
+    hbm = pl.BlockSpec(memory_space=pltpu.HBM)
     history = (dialogs, entries * PAGE, HD)
     return pl.pallas_call(
         functools.partial(attend_kernel, tensor_rows),
         out_shape=(out, out),
-        in_specs=[smem, smem, vmem, vmem, vmem, pl.BlockSpec(memory_space=pltpu.HBM)],
+        in_specs=[smem, smem, vmem, vmem, vmem, hbm],
         out_specs=(vmem, vmem),
         scratch_shapes=[
             pltpu.VMEM((dialogs, entries) + pages.shape[1:], jnp.float32),
             pltpu.VMEM(kv_new.shape, jnp.float32),
             pltpu.VMEM(history, jnp.bfloat16),
             pltpu.VMEM(history, jnp.bfloat16),
-            pltpu.VMEM((rows, weight.shape[0]), jnp.bfloat16),
-            pltpu.VMEM((panels, weight.shape[0], weight.shape[1] // panels), weight.dtype),
-            pltpu.SemaphoreType.DMA((panels,)),
+            pltpu.VMEM((2 * tensor_rows, rows // (2 * tensor_rows), weight.shape[0]), jnp.float32),
+            pltpu.VMEM((PANELS, weight.shape[0], weight.shape[1] // PANELS), weight.dtype),
+            pltpu.SemaphoreType.DMA((PANELS,)),
         ],
         compiler_params=pltpu.CompilerParams(vmem_limit_bytes=48 * 1024 * 1024),
         name="attend",
     )(place, hist_len, queries, kv_new, pages, weight)
+
+
+def sum_over_tensor(give, keep, tensor_rows):
+    swap = [(0, 1), (1, 0)]
+    beside = [(row, row ^ 1) for row in range(tensor_rows)]
+    across = [(row, tensor_rows - 1 - row) for row in range(tensor_rows)]
+    came = lax.ppermute(give, "core", swap)
+    half = give.shape[1] // 2
+    quarter = half // 2
+    wide = jnp.float32
+    near = keep[:, :half].astype(wide) + came[:, :half].astype(wide)
+    far = (keep[:, half:].astype(wide) + came[:, half:].astype(wide)).astype(give.dtype)
+    moved = (
+        lax.ppermute(far[0], "row", beside),
+        lax.ppermute(far[1], "row", across),
+    )
+    sums = [near[side] + moved[side].astype(wide) for side in range(2)]
+    last = (
+        lax.ppermute(sums[0][quarter:].astype(give.dtype), "row", across),
+        lax.ppermute(sums[1][quarter:].astype(give.dtype), "row", beside),
+    )
+    return jnp.concatenate(
+        [(sums[side][:quarter] + last[side].astype(wide)).astype(give.dtype) for side in range(2)],
+        axis=1,
+    )
 
 
 def local(queries, kv_new, pool, page_table, hist_len, o_weight):
@@ -231,11 +256,7 @@
     pages = pages.reshape(groups * SLOT, 2 * PAGE, HD)
     fresh = kv_new.reshape(2 * kv_new.shape[0], HD)
     give, keep = attend(place, hist_len, queries, fresh, pages, o_weight, tensor_rows)
-    came = lax.ppermute(give, "core", [(0, 1), (1, 0)])
-    pair = (keep.astype(jnp.float32) + came.astype(jnp.float32)).astype(jnp.bfloat16)
-    pair = pair.reshape(tensor_rows, -1, pair.shape[1])
-    blocks = lax.all_to_all(pair, "row", split_axis=0, concat_axis=0, tiled=True)
-    return jnp.sum(blocks.astype(jnp.float32), axis=0).astype(jnp.bfloat16)
+    return sum_over_tensor(give, keep, tensor_rows)
 
 
 def solution(mesh):

time: 87.3 us -> 87 us (level)
  blocking collectives: 70.5 us -> 56.5 us
  waiting for transfers between devices: 1.9 us -> 9.41 us
  starting transfers between devices: 0.09 us -> 6.32 us
    all_to_all x1 -> x0, blocking collectives: 14 us -> none  [local(): lax.all_to_all(pair, 'row', split_axis=0, concat_axis=0, tiled=True)]
    ppermute x1 -> x5, waiting for transfers between devices: 1.9 us -> 9.41 us  [the longest x1 2.51 us: sum_over_tensor(): lax.ppermute(far[1], 'row', across)]
    ppermute x1 -> x5, starting transfers between devices: 0.09 us -> 6.32 us  [the longest x1 2.31 us: sum_over_tensor(): lax.ppermute(sums[0][quarter:].astype(give.dtype), 'row', across)]
  transfers between devices with their start and end apart: 1 -> 5, of which waited for: 1 -> 5; matrix products, arithmetic and copies ran while one was open for 0% -> 0% of each run, Pallas kernels for 0% -> 0%
where the time goes in v3:
time: 87 us; the launch traced here: 86.8 us
  blocking collectives  56.5 us (65%)
  Pallas kernels  12.2 us (14%)
  waiting for transfers between devices  9.41 us (11%)
  starting transfers between devices  6.32 us (7%)
  local copies, waits for them, and re-layouts  1.39 us (2%)
  other arithmetic  0.87 us (1%)
    all_to_all x1, blocking collectives, local(): lax.all_to_all(sent, REPLICA, split_axis=0, concat_axis=0, tiled=True)  41.1 us
    all_to_all x1, blocking collectives, local(): lax.all_to_all(wanted, REPLICA, split_axis=0, concat_axis=0, tiled=True)  15.4 us
    pallas_call x1, Pallas kernels, attend(): pl.pallas_call(functools.partial(attend_kernel, tensor_rows), out_shape=(...  8.1 us
    pallas_call x1, Pallas kernels, plan(): pl.pallas_call(functools.partial(plan_kernel, groups), out_shape=(jax.Sha...  3.18 us
    ppermute x1, waiting for transfers between devices, sum_over_tensor(): lax.ppermute(far[1], 'row', across)  2.51 us
    ppermute x1, starting transfers between devices, sum_over_tensor(): lax.ppermute(sums[0][quarter:].astype(give.dtype), 'row', across)  2.31 us
    ppermute x1, starting transfers between devices, sum_over_tensor(): lax.ppermute(far[1], 'row', across)  2.18 us
    ppermute x1, waiting for transfers between devices, sum_over_tensor(): lax.ppermute(sums[1][quarter:].astype(give.dtype), 'row', beside)  1.92 us
  transfers between devices with their start and end apart: 5, of which 5 were waited for; matrix products, arithmetic and copies ran while one was open for 0% of the time, Pallas kernels for 0%

profile of v3, /device:TPU:0, one launch (start us, length us, event | category | flops | bytes accessed | tf_op | source)
XLA Modules:
  0.0 86.8 jit_solution(18330838261316811049)
XLA Ops:
  0.0 0.0 copy-start.2
  0.0 0.7 copy-done.2
  0.7 0.0 copy-start.4
  0.7 0.7 copy-done.4
  1.3 3.2 %plan.1 = (s32[16,1,128]{2,1,0:T(1,128)S(1)}, s32[2,12]{1,0:T(2,128)S(1)}, bf16[48,256,128]{2,1,0:T(8,128)(2,1)S(1)}) custom-call(s32[2,12]{1,0:T(2,128)S(1)} %copy-done.4, s32[2]{0:T(128)S(1)} %copy-done.2, bf16[48,256,128]{2,1,0:T(8,128)(2,1)} %bitcast.17), custom_call_target="tpu_custom_call" | custom-call | tf_op jit(solution)/shard_map/plan/pallas_call | solution.py:50
  4.5 15.4 %all_to_all.10.asked = s32[16,1,128]{2,1,0:T(1,128)S(1)} all-to-all(s32[16,1,128]{2,1,0:T(1,128)S(1)} %get-tuple-element.11), channel_id=1, replica_groups=mesh['replica_0'=4,'replica_1'=4,'row'=4,'core'=2] {'replica_0','replica..., dimensions={0} | all-to-all | bytes 16384 | tf_op jit(solution)/shard_map/all_to_all | solution.py:253
  19.9 0.9 %collect.1 = bf16[16,3,256,128]{3,2,1,0:T(8,128)(2,1)S(1)} custom-call(s32[16,1,128]{2,1,0:T(1,128)S(1)} %all_to_all.10.asked, bf16[48,256,128]{2,1,0:T(8,128)(2,1)S(1)} %get-tuple-element.12.pool), custom_call_target="tpu_custom_call" | custom-call | tf_op jit(solution)/shard_map/collect/pallas_call | solution.py:77
  20.8 0.0 copy-start
  20.8 0.0 copy-start.1
  20.8 0.0 copy-start.3
  20.8 41.1 %all_to_all.11 = bf16[16,3,256,128]{3,2,1,0:T(8,128)(2,1)S(1)} all-to-all(bf16[16,3,256,128]{3,2,1,0:T(8,128)(2,1)S(1)} %collect.1), channel_id=1, replica_groups=mesh['replica_0'=4,'replica_1'=4,'row'=4,'core'=2] {'replica_0','replica..., dimensions={0} | all-to-all | bytes 6291456 | tf_op jit(solution)/shard_map/all_to_all | solution.py:255
  62.0 0.0 copy-done
  62.0 0.0 copy-done.1
  62.0 0.0 copy-done.3
  62.0 8.1 %attend.1 = (bf16[2,32,4096]{2,1,0:T(8,128)(2,1)S(1)}, bf16[2,32,4096]{2,1,0:T(8,128)(2,1)S(1)}) custom-call(s32[2,12]{1,0:T(2,128)S(1)} %get-tuple-element.10.place, s32[2]{0:T(128)S(1)} %copy-done.3, bf16[64,1024]{1,0:T(8,128)(2,1)S(1)} %copy-done, bf16[128,128]{1,0:T(8,128)(2,1)S(1)} %bitcast.16, bf16[48,256,128]{2,1,0:T(8,128)(2,1)S(1)} %bitcast.15, ...), custom_call_target="tpu_custom_call" | custom-call | tf_op jit(solution)/shard_map/attend/pallas_call | solution.py:204
  70.1 0.1 collective-permute-start
  70.2 1.9 %collective-permute-done = bf16[2,32,4096]{2,1,0:T(8,128)(2,1)S(1)} collective-permute-done((bf16[2,32,4096]{2,1,0:T(8,128)(2,1)S(1)}, bf16[2,32,4096]{2,1,0:T(8,128)(2,1)S(1)}, u32[]{:S(2)}, u32[]{:S(2)}) %collective-permute-start) | collective-permute-done | bytes 524320 | tf_op jit(solution)/shard_map/ppermute | solution.py:227
  72.1 0.1 add_convert_fusion
  72.2 1.7 %collective-permute-start.1 = (bf16[16,4096]{1,0:T(8,128)(2,1)S(1)}, bf16[16,4096]{1,0:T(8,128)(2,1)S(1)}, u32[]{:S(2)}, u32[]{:S(2)}) collective-permute-start(bf16[16,4096]{1,0:T(8,128)(2,1)S(1)} %get-tuple-element.19), channel_id=1, source_target_pairs={{0,2},{2,0},{4,6},{6,4},{1,3},{3,1},{5,7},{7,5},{8,10},{10,8},{12,... | collective-permute-start | bytes 393224 | tf_op jit(solution)/shard_map/ppermute | solution.py:234
  73.9 2.2 %collective-permute-start.3 = (bf16[16,4096]{1,0:T(8,128)(2,1)S(1)}, bf16[16,4096]{1,0:T(8,128)(2,1)S(1)}, u32[]{:S(2)}, u32[]{:S(2)}) collective-permute-start(bf16[16,4096]{1,0:T(8,128)(2,1)S(1)} %get-tuple-element.20), channel_id=1, source_target_pairs={{0,6},{2,4},{4,2},{6,0},{1,7},{3,5},{5,3},{7,1},{8,14},{10,12},{12... | collective-permute-start | bytes 393224 | tf_op jit(solution)/shard_map/ppermute | solution.py:235
  76.0 1.8 %collective-permute-done.1 = bf16[16,4096]{1,0:T(8,128)(2,1)S(1)} collective-permute-done((bf16[16,4096]{1,0:T(8,128)(2,1)S(1)}, bf16[16,4096]{1,0:T(8,128)(2,1)S(1)}, u32[]{:S(2)}, u32[]{:S(2)}) %collective-permute-start.1) | collective-permute-done | bytes 131104 | tf_op jit(solution)/shard_map/ppermute | solution.py:234
  77.8 2.5 %collective-permute-done.3 = bf16[16,4096]{1,0:T(8,128)(2,1)S(1)} collective-permute-done((bf16[16,4096]{1,0:T(8,128)(2,1)S(1)}, bf16[16,4096]{1,0:T(8,128)(2,1)S(1)}, u32[]{:S(2)}, u32[]{:S(2)}) %collective-permute-start.3) | collective-permute-done | bytes 131104 | tf_op jit(solution)/shard_map/ppermute | solution.py:235
  80.3 0.1 fusion.1
  80.4 0.1 collective-permute-start.4
  80.5 2.3 %collective-permute-start.2 = (bf16[8,4096]{1,0:T(8,128)(2,1)S(1)}, bf16[8,4096]{1,0:T(8,128)(2,1)S(1)}, u32[]{:S(2)}, u32[]{:S(2)}) collective-permute-start(bf16[8,4096]{1,0:T(8,128)(2,1)S(1)} %slice.81), channel_id=1, source_target_pairs={{0,6},{2,4},{4,2},{6,0},{1,7},{3,5},{5,3},{7,1},{8,14},{10,12},{12... | collective-permute-start | bytes 196616 | tf_op jit(solution)/shard_map/ppermute | solution.py:239
  82.8 1.9 %collective-permute-done.4 = bf16[8,4096]{1,0:T(8,128)(2,1)S(1)} collective-permute-done((bf16[8,4096]{1,0:T(8,128)(2,1)S(1)}, bf16[8,4096]{1,0:T(8,128)(2,1)S(1)}, u32[]{:S(2)}, u32[]{:S(2)}) %collective-permute-start.4) | collective-permute-done | bytes 65568 | tf_op jit(solution)/shard_map/ppermute | solution.py:240
  84.8 1.3 %collective-permute-done.2 = bf16[8,4096]{1,0:T(8,128)(2,1)S(1)} collective-permute-done((bf16[8,4096]{1,0:T(8,128)(2,1)S(1)}, bf16[8,4096]{1,0:T(8,128)(2,1)S(1)}, u32[]{:S(2)}, u32[]{:S(2)}) %collective-permute-start.2) | collective-permute-done | bytes 65568 | tf_op jit(solution)/shard_map/ppermute | solution.py:239
  86.1 0.7 pad_maximum_fusion
  (5 shorter events, 0.1 us)
Async XLA Ops:
  0.0 0.7 copy-start.2
  0.7 0.7 copy-start.4
  20.8 41.2 %copy-start = (bf16[64,1024]{1,0:T(8,128)(2,1)S(1)}, bf16[64,1024]{1,0:T(8,128)(2,1)}, u32[]{:S(2)}) copy-start(bf16[64,1024]{1,0:T(8,128)(2,1)} %queries.1) | copy-start | bytes 393220
  20.8 41.2 %copy-start.1 = (bf16[64,2,128]{2,1,0:T(2,128)(2,1)S(1)}, bf16[64,2,128]{2,1,0:T(2,128)(2,1)}, u32[]{:S(2)}) copy-start(bf16[64,2,128]{2,1,0:T(2,128)(2,1)} %param.7) | copy-start | bytes 98308
  20.8 41.1 %copy-start.3 = (s32[2]{0:T(128)S(1)}, s32[2]{0:T(128)}, u32[]{:S(2)}) copy-start(s32[2]{0:T(128)} %length.3) | copy-start | bytes 28
  70.1 2.0 %collective-permute-start = (bf16[2,32,4096]{2,1,0:T(8,128)(2,1)S(1)}, bf16[2,32,4096]{2,1,0:T(8,128)(2,1)S(1)}, u32[]{:S(2)}, u32[]{:S(2)}) collective-permute-start(bf16[2,32,4096]{2,1,0:T(8,128)(2,1)S(1)} %get-tuple-element.14), channel_id=1, source_target_pairs={{0,1},{1,0},{2,3},{3,2},{4,5},{5,4},{6,7},{7,6},{8,9},{9,8},{10,11... | collective-permute-start | bytes 1572872 | tf_op jit(solution)/shard_map/ppermute | solution.py:227
  72.2 5.6 %collective-permute-start.1 = (bf16[16,4096]{1,0:T(8,128)(2,1)S(1)}, bf16[16,4096]{1,0:T(8,128)(2,1)S(1)}, u32[]{:S(2)}, u32[]{:S(2)}) collective-permute-start(bf16[16,4096]{1,0:T(8,128)(2,1)S(1)} %get-tuple-element.19), channel_id=1, source_target_pairs={{0,2},{2,0},{4,6},{6,4},{1,3},{3,1},{5,7},{7,5},{8,10},{10,8},{12,... | collective-permute-start | bytes 393224 | tf_op jit(solution)/shard_map/ppermute | solution.py:234
  73.9 6.5 %collective-permute-start.3 = (bf16[16,4096]{1,0:T(8,128)(2,1)S(1)}, bf16[16,4096]{1,0:T(8,128)(2,1)S(1)}, u32[]{:S(2)}, u32[]{:S(2)}) collective-permute-start(bf16[16,4096]{1,0:T(8,128)(2,1)S(1)} %get-tuple-element.20), channel_id=1, source_target_pairs={{0,6},{2,4},{4,2},{6,0},{1,7},{3,5},{5,3},{7,1},{8,14},{10,12},{12... | collective-permute-start | bytes 393224 | tf_op jit(solution)/shard_map/ppermute | solution.py:235
  80.4 4.3 %collective-permute-start.4 = (bf16[8,4096]{1,0:T(8,128)(2,1)S(1)}, bf16[8,4096]{1,0:T(8,128)(2,1)S(1)}, u32[]{:S(2)}, u32[]{:S(2)}) collective-permute-start(bf16[8,4096]{1,0:T(8,128)(2,1)S(1)} %slice.80), channel_id=1, source_target_pairs={{0,2},{2,0},{4,6},{6,4},{1,3},{3,1},{5,7},{7,5},{8,10},{10,8},{12,... | collective-permute-start | bytes 196616 | tf_op jit(solution)/shard_map/ppermute | solution.py:240
  80.5 5.6 %collective-permute-start.2 = (bf16[8,4096]{1,0:T(8,128)(2,1)S(1)}, bf16[8,4096]{1,0:T(8,128)(2,1)S(1)}, u32[]{:S(2)}, u32[]{:S(2)}) collective-permute-start(bf16[8,4096]{1,0:T(8,128)(2,1)S(1)} %slice.81), channel_id=1, source_target_pairs={{0,6},{2,4},{4,2},{6,0},{1,7},{3,5},{5,3},{7,1},{8,14},{10,12},{12... | collective-permute-start | bytes 196616 | tf_op jit(solution)/shard_map/ppermute | solution.py:239
